TPU v7x, 32 devices: a whole 2x2x4 slice. The times are simulated.
32 devices in a mesh: groups: 2 (over y), rows: 4 (over z), sub: 4 (over x, core).
Axes of the slice: x: 2, y: 2, z: 4, core: 2. Of those that a mesh axis runs over, the one named last changes fastest.
Arguments:
- matrix: float32 [16384, 1024], P(('groups', 'rows', 'sub')), parts along dimension 0
- sign_bits: int32 [16384], P(('groups', 'rows', 'sub')), parts along dimension 0, may hold values from 0 to 1
- samples: int32 [8192], P('groups'), parts along dimension 0, may hold values from 0 to 8191
Outputs:
- cholesky_factor: float32 [2048, 1024], P('groups'), parts along dimension 0
There are 2 independent parts, one for each index of `groups`. A program takes and returns all parts, laid end to end along the dimension named above; each array names one. Nothing has to cross between parts.
Inputs may be any that keep to these rules, and one draw needn't show every extreme that they name: `samples`: row numbers of the whole matrix, drawn independently; a row may be drawn more than once.
All inputs are finite; a program needn't handle non-finite values.
Results may differ from a plain program's by a relative error of at most 0.00011.
Values sent between devices are 32-bit elements; how exact they have to be, the bound alone decides.
A program may use at most 64 MiB of HBM per device.

v0:
```python
import jax
import jax.numpy as jnp
from jax import lax
from jax.sharding import PartitionSpec as P

HIGHEST = lax.Precision.HIGHEST


def hadamard_table(extent):
    line_ids = jnp.arange(extent, dtype=jnp.int32)
    correlation = jnp.bitwise_and(line_ids[:, None], line_ids[None, :])
    parity = jnp.zeros((extent, extent), jnp.int32)
    for bit_pos in range(extent.bit_length() - 1):
        parity = parity + jnp.bitwise_and(jnp.right_shift(correlation, bit_pos), 1)
    return (1 - 2 * (parity % 2)).astype(jnp.float32)


def local_transform(values):
    rows_here, columns = values.shape
    inner_size = min(rows_here, 128)
    outer_size = rows_here // inner_size
    blocks = values.reshape(outer_size, inner_size, columns)
    blocks = jnp.einsum("ab,qbn->qan", hadamard_table(inner_size), blocks, precision=HIGHEST)
    blocks = jnp.einsum("pq,qan->pan", hadamard_table(outer_size), blocks, precision=HIGHEST)
    return blocks.reshape(rows_here, columns)


def mix_sources(received):
    return jnp.einsum("ab,bjn->ajn", hadamard_table(received.shape[0]), received, precision=HIGHEST)


def body(matrix, sign_bits, samples):
    rows_here, columns = matrix.shape
    devices = lax.axis_size(("rows", "sub"))
    position = lax.axis_index(("rows", "sub"))
    per_block = rows_here // devices
    sign_values = (2 * sign_bits - 1).astype(jnp.float32)
    current = local_transform(matrix * sign_values[:, None])
    block_ids = (
        (jnp.arange(devices, dtype=jnp.int32) * rows_here)[:, None]
        + position * per_block
        + jnp.arange(per_block, dtype=jnp.int32)[None, :]
    )
    blocks = current.reshape(devices, per_block, columns)
    mixed_rows = mix_sources(
        lax.all_to_all(blocks, ("rows", "sub"), split_axis=0, concat_axis=0, tiled=True)
    )
    owned_rows = mixed_rows.reshape(rows_here, columns)
    row_ids = block_ids.reshape(rows_here)
    matches = (row_ids[:, None] == samples[None, :]).astype(jnp.float32)
    counts = jnp.sum(matches, axis=1)
    weighted = owned_rows * counts[:, None]
    total_rows = rows_here * devices
    own_terms = jnp.einsum("rn,rm->nm", weighted, owned_rows, precision=HIGHEST) / jnp.float32(
        total_rows * samples.shape[0]
    )
    gram_matrix = lax.psum(own_terms, ("rows", "sub"))
    return jnp.linalg.cholesky(gram_matrix)


def solution(mesh):
    placed = (P(("groups", "rows", "sub"), None), P(("groups", "rows", "sub")), P("groups"))
    return jax.shard_map(
        body, mesh=mesh, in_specs=placed, out_specs=P("groups", None), check_vma=False
    )
```

profile of v0, /device:TPU:0, one launch (start us, length us, event | category | flops | bytes accessed | tf_op | source)
XLA Modules:
  0.0 427.4 jit_solution(5437568680601087725)
XLA Ops:
  9.0 3.5 convolution_bitcast_fusion
  14.5 5.4 %fusion.69 = f32[4,128,1024]{2,0,1:T(4,128)S(1)} fusion(f32[4,128,1024]{2,0,1:T(4,128)} %copy.23), kind=kOutput, calls=%fused_computation.112 | convolution fusion | flops 25166144 | bytes 4194304 | tf_op jit(solution)/shard_map/pq,qan->pan/dot_general | solution.py:24
  22.4 7.4 %all-to-all-start = ((f32[16,32,1024]{2,1,0:T(8,128)}), f32[16,32,1024]{2,1,0:T(8,128)S(1)}, u32[]{:S(2)}, u32[]{:S(2)}) async-start(f32[16,32,1024]{2,1,0:T(8,128)} %bitcast.60), calls=%async_computation | async-start | bytes 4194304 | tf_op jit(solution)/shard_map/all_to_all | solution.py:46
  31.7 39.1 %all-to-all-done = f32[16,32,1024]{2,1,0:T(8,128)S(1)} async-done(((f32[16,32,1024]{2,1,0:T(8,128)}), f32[16,32,1024]{2,1,0:T(8,128)S(1)}, u32[]{:S(2)}, u32[]{:S(2)}) %all-to-all-start) | async-done | bytes 2097184 | tf_op jit(solution)/shard_map/all_to_all | solution.py:46
  73.7 8.9 %bitcast_multiply_fusion = f32[1024,1024]{0,1:T(8,128)} fusion(f32[16,32,1024]{2,0,1:T(8,128)S(1)} %fusion.5, f32[16,32]{0,1:T(8,128)S(1)} %copy.26), kind=kOutput, calls=%fused_computation.3 | convolution fusion | flops 6444023808 | bytes 6293504 | tf_op jit(solution)/shard_map/rn,rm->nm/dot_general | solution.py:54
  82.6 118.0 %all-reduce.3.cloned.1.call-done = f32[1024,1024]{0,1:T(8,128)} async-done(((f32[1024,1024]{0,1:T(8,128)}), f32[1024,1024]{0,1:T(8,128)}) %all-reduce.3.cloned.1.call-update) | async-done | bytes 4194320 | tf_op jit(solution)/shard_map/psum | solution.py:57
  200.6 5.5 %copy.28 = f32[1024,1024]{1,0:T(8,128)} copy(f32[1024,1024]{0,1:T(8,128)} %all-reduce.3.cloned.1.call-done) | data formatting | bytes 8388608 | tf_op jit(solution)/shard_map/psum | solution.py:57
  206.1 4.4 %fusion = f32[1024,1024]{1,0:T(8,128)S(1)} fusion(f32[1024,1024]{1,0:T(8,128)} %copy.28, f32[1024,1024]{0,1:T(8,128)} %all-reduce.3.cloned.1.call-done), kind=kLoop, calls=%fused_computation.2 | loop fusion | flops 2097152 | bytes 12582912 | tf_op jit(solution)/shard_map/jit(cholesky)/div | solution.py:58
  212.5 11.7 %cholesky.223 = f32[128,128]{1,0:T(8,128)S(1)} custom-call(f32[128,128]{1,0:T(8,128)S(1)} %cholesky.580), custom_call_target="Cholesky" | custom-call | tf_op jit(solution)/shard_map/jit(cholesky)/cholesky | solution.py:58
  224.2 9.8 %custom-call.59 = f32[1,128,128]{1,2,0:T(8,128)S(1)} custom-call(f32[1,128,128]{2,1,0:T(8,128)S(1)} %get-tuple-element.26), custom_call_target="InvertDiagBlocksLowerTriangular" | custom-call | tf_op jit(solution)/shard_map/jit(cholesky)/cholesky | solution.py:58
  240.4 11.9 %cholesky.244 = f32[128,128]{1,0:T(8,128)S(1)} custom-call(f32[128,128]{1,0:T(8,128)S(1)} %cholesky.584), custom_call_target="Cholesky" | custom-call | tf_op jit(solution)/shard_map/jit(cholesky)/cholesky | solution.py:58
  253.0 9.8 %custom-call.60 = f32[1,128,128]{1,2,0:T(8,128)S(1)} custom-call(f32[1,128,128]{2,1,0:T(8,128)S(1)} %get-tuple-element.23), custom_call_target="InvertDiagBlocksLowerTriangular" | custom-call | tf_op jit(solution)/shard_map/jit(cholesky)/cholesky | solution.py:58
  266.1 11.7 %cholesky.468 = f32[128,128]{1,0:T(8,128)S(1)} custom-call(f32[128,128]{1,0:T(8,128)S(1)} %cholesky.589), custom_call_target="Cholesky" | custom-call | tf_op jit(solution)/shard_map/jit(cholesky)/cholesky | solution.py:58
  279.1 9.8 %custom-call.61 = f32[1,128,128]{1,2,0:T(8,128)S(1)} custom-call(f32[1,128,128]{2,1,0:T(8,128)S(1)} %get-tuple-element.20), custom_call_target="InvertDiagBlocksLowerTriangular" | custom-call | tf_op jit(solution)/shard_map/jit(cholesky)/cholesky | solution.py:58
  292.4 12.1 %cholesky.487 = f32[128,128]{1,0:T(8,128)S(1)} custom-call(f32[128,128]{1,0:T(8,128)S(1)} %cholesky.594), custom_call_target="Cholesky" | custom-call | tf_op jit(solution)/shard_map/jit(cholesky)/cholesky | solution.py:58
  305.8 9.8 %custom-call.62 = f32[1,128,128]{1,2,0:T(8,128)S(1)} custom-call(f32[1,128,128]{2,1,0:T(8,128)S(1)} %get-tuple-element.17), custom_call_target="InvertDiagBlocksLowerTriangular" | custom-call | tf_op jit(solution)/shard_map/jit(cholesky)/cholesky | solution.py:58
  319.1 11.7 %cholesky.506 = f32[128,128]{1,0:T(8,128)S(1)} custom-call(f32[128,128]{1,0:T(8,128)S(1)} %cholesky.599), custom_call_target="Cholesky" | custom-call | tf_op jit(solution)/shard_map/jit(cholesky)/cholesky | solution.py:58
  332.1 10.0 %custom-call.63 = f32[1,128,128]{1,2,0:T(8,128)S(1)} custom-call(f32[1,128,128]{2,1,0:T(8,128)S(1)} %get-tuple-element.14), custom_call_target="InvertDiagBlocksLowerTriangular" | custom-call | tf_op jit(solution)/shard_map/jit(cholesky)/cholesky | solution.py:58
  345.4 11.7 %cholesky.526 = f32[128,128]{1,0:T(8,128)S(1)} custom-call(f32[128,128]{1,0:T(8,128)S(1)} %cholesky.604), custom_call_target="Cholesky" | custom-call | tf_op jit(solution)/shard_map/jit(cholesky)/cholesky | solution.py:58
  358.4 9.8 %custom-call.64 = f32[1,128,128]{1,2,0:T(8,128)S(1)} custom-call(f32[1,128,128]{2,1,0:T(8,128)S(1)} %get-tuple-element.11), custom_call_target="InvertDiagBlocksLowerTriangular" | custom-call | tf_op jit(solution)/shard_map/jit(cholesky)/cholesky | solution.py:58
  371.2 11.9 %cholesky.546 = f32[128,128]{1,0:T(8,128)S(1)} custom-call(f32[128,128]{1,0:T(8,128)S(1)} %cholesky.609), custom_call_target="Cholesky" | custom-call | tf_op jit(solution)/shard_map/jit(cholesky)/cholesky | solution.py:58
  384.4 9.8 %custom-call.65 = f32[1,128,128]{1,2,0:T(8,128)S(1)} custom-call(f32[1,128,128]{2,1,0:T(8,128)S(1)} %get-tuple-element.8), custom_call_target="InvertDiagBlocksLowerTriangular" | custom-call | tf_op jit(solution)/shard_map/jit(cholesky)/cholesky | solution.py:58
  396.8 11.7 %cholesky.564 = f32[128,128]{1,0:T(8,128)S(1)} custom-call(f32[128,128]{1,0:T(8,128)S(1)} %convolution_subtract_fusion.6), custom_call_target="Cholesky" | custom-call | tf_op jit(solution)/shard_map/jit(cholesky)/cholesky | solution.py:58
  415.5 4.9 %select_select_fusion = f32[1024,1024]{1,0:T(8,128)} fusion(f32[1024,1024]{1,0:T(8,128)} %get-tuple-element.6, pred[]{:T(512)S(6)} %cholesky.579), kind=kLoop, calls=%fused_computation.4 | loop fusion | flops 3145728 | bytes 8388609 | tf_op jit(solution)/shard_map/jit(cholesky)/select_n | solution.py:58
  (54 shorter events, 48.3 us)
Async XLA Ops:
  19.9 10.6 %copy-start.1 = (s32[4096]{0:T(1024)S(1)}, s32[4096]{0:T(1024)}, u32[]{:S(2)}) copy-start(s32[4096]{0:T(1024)} %param.5) | copy-start | bytes 49156
  22.4 48.4 %all-to-all-start = ((f32[16,32,1024]{2,1,0:T(8,128)}), f32[16,32,1024]{2,1,0:T(8,128)S(1)}, u32[]{:S(2)}, u32[]{:S(2)}) async-start(f32[16,32,1024]{2,1,0:T(8,128)} %bitcast.60), calls=%async_computation | async-start | bytes 4194304 | tf_op jit(solution)/shard_map/all_to_all | solution.py:46
  29.8 170.8 %all-reduce.3.cloned.1.call-start = ((), (), s32[]{:S(2)}) async-start(), calls=%async_computation.1 | async-start | bytes 8388608 | tf_op jit(solution)/shard_map/psum | solution.py:57
  210.5 1.9 copy-start
Sparse Core Ops, SparseCore 0:
  82.7 117.8 all-reduce.2
where the time goes:
time: 435 us; the launch traced here: 427 us
  other arithmetic  185 us (43%)
  waiting for transfers between devices  157 us (36%)
  matrix products  43.5 us (10%)
  between operations  18.8 us (4%)
  local copies, waits for them, and re-layouts  14.7 us (3%)
  starting transfers between devices  7.89 us (2%)
    another operation x30, other arithmetic, body(): return jnp.linalg.cholesky(gram_matrix)  172 us
    psum x1, waiting for transfers between devices, body(): gram_matrix = lax.psum(own_terms, ('rows', 'sub'))  118 us
    all_to_all x1, waiting for transfers between devices, body(): lax.all_to_all(blocks, ('rows', 'sub'), split_axis=0, concat_axis=0, tile...  39.1 us
    another operation x14, matrix products, body(): return jnp.linalg.cholesky(gram_matrix)  22.9 us
    dot_general x1, matrix products, body(): jnp.einsum('rn,rm->nm', weighted, owned_rows, precision=HIGHEST)  8.89 us
  transfers between devices with their start and end apart: 2, of which 2 were waited for; matrix products, arithmetic and copies ran while one was open for 0% of the time, Pallas kernels for 0%

commit v1 on v0

--- a/solution.py
+++ b/solution.py
@@ -54,7 +54,9 @@
     own_terms = jnp.einsum("rn,rm->nm", weighted, owned_rows, precision=HIGHEST) / jnp.float32(
         total_rows * samples.shape[0]
     )
-    gram_matrix = lax.psum(own_terms, ("rows", "sub"))
+    gram_matrix = own_terms
+    for mesh_axis in ("sub", "rows"):
+        gram_matrix = lax.psum(gram_matrix, mesh_axis)
     return jnp.linalg.cholesky(gram_matrix)
 
 

time: 435 us -> 567 us (1.30)
  waiting for transfers between devices: 157 us -> 289 us
    psum x1 -> x2, waiting for transfers between devices: 118 us -> 250 us  [body(): gram_matrix = lax.psum(gram_matrix, mesh_axis)]
  transfers between devices with their start and end apart: 2 -> 3, of which waited for: 2 -> 3; matrix products, arithmetic and copies ran while one was open for 0% -> 0% of each run, Pallas kernels for 0% -> 0%
where the time goes in v1:
time: 567 us; the launch traced here: 559 us
  waiting for transfers between devices  289 us (51%)
  other arithmetic  185 us (33%)
  matrix products  43.5 us (8%)
  between operations  18.8 us (3%)
  local copies, waits for them, and re-layouts  14.7 us (3%)
  starting transfers between devices  7.93 us (1%)
    psum x2, waiting for transfers between devices, body(): gram_matrix = lax.psum(gram_matrix, mesh_axis)  250 us
    another operation x30, other arithmetic, body(): return jnp.linalg.cholesky(gram_matrix)  172 us
    all_to_all x1, waiting for transfers between devices, body(): lax.all_to_all(blocks, ('rows', 'sub'), split_axis=0, concat_axis=0, tile...  39.1 us
    another operation x14, matrix products, body(): return jnp.linalg.cholesky(gram_matrix)  22.9 us
  transfers between devices with their start and end apart: 3, of which 3 were waited for; matrix products, arithmetic and copies ran while one was open for 0% of the time, Pallas kernels for 0%

profile of v1, /device:TPU:0, one launch (start us, length us, event | category | flops | bytes accessed | tf_op | source)
XLA Modules:
  0.0 559.1 jit_solution(2820878943944639255)
XLA Ops:
  14.5 5.4 fusion.69
  22.4 7.4 %all-to-all-start = ((f32[16,32,1024]{2,1,0:T(8,128)}), f32[16,32,1024]{2,1,0:T(8,128)S(1)}, u32[]{:S(2)}, u32[]{:S(2)}) async-start(f32[16,32,1024]{2,1,0:T(8,128)} %bitcast.60), calls=%async_computation | async-start | bytes 4194304 | tf_op jit(solution)/shard_map/all_to_all | solution.py:46
  31.7 39.1 %all-to-all-done = f32[16,32,1024]{2,1,0:T(8,128)S(1)} async-done(((f32[16,32,1024]{2,1,0:T(8,128)}), f32[16,32,1024]{2,1,0:T(8,128)S(1)}, u32[]{:S(2)}, u32[]{:S(2)}) %all-to-all-start) | async-done | bytes 2097184 | tf_op jit(solution)/shard_map/all_to_all | solution.py:46
  73.7 8.9 %bitcast_multiply_fusion = f32[1024,1024]{0,1:T(8,128)} fusion(f32[16,32,1024]{2,0,1:T(8,128)S(1)} %fusion.5, f32[16,32]{0,1:T(8,128)S(1)} %copy.26), kind=kOutput, calls=%fused_computation.3 | convolution fusion | flops 6444023808 | bytes 6293504 | tf_op jit(solution)/shard_map/rn,rm->nm/dot_general | solution.py:54
  82.6 92.2 %all-reduce.4.cloned.1.call-done = f32[1024,1024]{0,1:T(8,128)} async-done(((f32[1024,1024]{0,1:T(8,128)}), f32[1024,1024]{0,1:T(8,128)}) %all-reduce.4.cloned.1.call-update) | async-done | bytes 4194320 | tf_op jit(solution)/shard_map/psum | solution.py:59
  174.8 157.5 %all-reduce.6.cloned.1.call-done = f32[1024,1024]{0,1:T(8,128)} async-done(((f32[1024,1024]{0,1:T(8,128)}), f32[1024,1024]{0,1:T(8,128)}) %all-reduce.6.cloned.1.call-update) | async-done | bytes 4194320 | tf_op jit(solution)/shard_map/psum | solution.py:59
  332.3 5.5 copy.28
  337.8 4.4 fusion
  344.2 11.7 %cholesky.223 = f32[128,128]{1,0:T(8,128)S(1)} custom-call(f32[128,128]{1,0:T(8,128)S(1)} %cholesky.580), custom_call_target="Cholesky" | custom-call | tf_op jit(solution)/shard_map/jit(cholesky)/cholesky | solution.py:60
  356.0 9.8 %custom-call.59 = f32[1,128,128]{1,2,0:T(8,128)S(1)} custom-call(f32[1,128,128]{2,1,0:T(8,128)S(1)} %get-tuple-element.26), custom_call_target="InvertDiagBlocksLowerTriangular" | custom-call | tf_op jit(solution)/shard_map/jit(cholesky)/cholesky | solution.py:60
  372.2 11.9 %cholesky.244 = f32[128,128]{1,0:T(8,128)S(1)} custom-call(f32[128,128]{1,0:T(8,128)S(1)} %cholesky.584), custom_call_target="Cholesky" | custom-call | tf_op jit(solution)/shard_map/jit(cholesky)/cholesky | solution.py:60
  384.7 9.8 %custom-call.60 = f32[1,128,128]{1,2,0:T(8,128)S(1)} custom-call(f32[1,128,128]{2,1,0:T(8,128)S(1)} %get-tuple-element.23), custom_call_target="InvertDiagBlocksLowerTriangular" | custom-call | tf_op jit(solution)/shard_map/jit(cholesky)/cholesky | solution.py:60
  397.9 11.7 %cholesky.468 = f32[128,128]{1,0:T(8,128)S(1)} custom-call(f32[128,128]{1,0:T(8,128)S(1)} %cholesky.589), custom_call_target="Cholesky" | custom-call | tf_op jit(solution)/shard_map/jit(cholesky)/cholesky | solution.py:60
  410.9 9.8 %custom-call.61 = f32[1,128,128]{1,2,0:T(8,128)S(1)} custom-call(f32[1,128,128]{2,1,0:T(8,128)S(1)} %get-tuple-element.20), custom_call_target="InvertDiagBlocksLowerTriangular" | custom-call | tf_op jit(solution)/shard_map/jit(cholesky)/cholesky | solution.py:60
  424.2 12.1 %cholesky.487 = f32[128,128]{1,0:T(8,128)S(1)} custom-call(f32[128,128]{1,0:T(8,128)S(1)} %cholesky.594), custom_call_target="Cholesky" | custom-call | tf_op jit(solution)/shard_map/jit(cholesky)/cholesky | solution.py:60
  437.6 9.8 %custom-call.62 = f32[1,128,128]{1,2,0:T(8,128)S(1)} custom-call(f32[1,128,128]{2,1,0:T(8,128)S(1)} %get-tuple-element.17), custom_call_target="InvertDiagBlocksLowerTriangular" | custom-call | tf_op jit(solution)/shard_map/jit(cholesky)/cholesky | solution.py:60
  450.8 11.7 %cholesky.506 = f32[128,128]{1,0:T(8,128)S(1)} custom-call(f32[128,128]{1,0:T(8,128)S(1)} %cholesky.599), custom_call_target="Cholesky" | custom-call | tf_op jit(solution)/shard_map/jit(cholesky)/cholesky | solution.py:60
  463.9 10.0 %custom-call.63 = f32[1,128,128]{1,2,0:T(8,128)S(1)} custom-call(f32[1,128,128]{2,1,0:T(8,128)S(1)} %get-tuple-element.14), custom_call_target="InvertDiagBlocksLowerTriangular" | custom-call | tf_op jit(solution)/shard_map/jit(cholesky)/cholesky | solution.py:60
  477.2 11.7 %cholesky.526 = f32[128,128]{1,0:T(8,128)S(1)} custom-call(f32[128,128]{1,0:T(8,128)S(1)} %cholesky.604), custom_call_target="Cholesky" | custom-call | tf_op jit(solution)/shard_map/jit(cholesky)/cholesky | solution.py:60
  490.2 9.8 %custom-call.64 = f32[1,128,128]{1,2,0:T(8,128)S(1)} custom-call(f32[1,128,128]{2,1,0:T(8,128)S(1)} %get-tuple-element.11), custom_call_target="InvertDiagBlocksLowerTriangular" | custom-call | tf_op jit(solution)/shard_map/jit(cholesky)/cholesky | solution.py:60
  502.9 11.9 %cholesky.546 = f32[128,128]{1,0:T(8,128)S(1)} custom-call(f32[128,128]{1,0:T(8,128)S(1)} %cholesky.609), custom_call_target="Cholesky" | custom-call | tf_op jit(solution)/shard_map/jit(cholesky)/cholesky | solution.py:60
  516.1 9.8 %custom-call.65 = f32[1,128,128]{1,2,0:T(8,128)S(1)} custom-call(f32[1,128,128]{2,1,0:T(8,128)S(1)} %get-tuple-element.8), custom_call_target="InvertDiagBlocksLowerTriangular" | custom-call | tf_op jit(solution)/shard_map/jit(cholesky)/cholesky | solution.py:60
  528.6 11.7 %cholesky.564 = f32[128,128]{1,0:T(8,128)S(1)} custom-call(f32[128,128]{1,0:T(8,128)S(1)} %convolution_subtract_fusion.6), custom_call_target="Cholesky" | custom-call | tf_op jit(solution)/shard_map/jit(cholesky)/cholesky | solution.py:60
  547.2 4.9 select_select_fusion
  (57 shorter events, 51.8 us)
Async XLA Ops:
  19.9 10.6 %copy-start.1 = (s32[4096]{0:T(1024)S(1)}, s32[4096]{0:T(1024)}, u32[]{:S(2)}) copy-start(s32[4096]{0:T(1024)} %param.5) | copy-start | bytes 49156
  22.4 48.4 %all-to-all-start = ((f32[16,32,1024]{2,1,0:T(8,128)}), f32[16,32,1024]{2,1,0:T(8,128)S(1)}, u32[]{:S(2)}, u32[]{:S(2)}) async-start(f32[16,32,1024]{2,1,0:T(8,128)} %bitcast.60), calls=%async_computation | async-start | bytes 4194304 | tf_op jit(solution)/shard_map/all_to_all | solution.py:46
  29.8 145.0 %all-reduce.4.cloned.1.call-start = ((), (), s32[]{:S(2)}) async-start(), calls=%async_computation.1 | async-start | bytes 8388608 | tf_op jit(solution)/shard_map/psum | solution.py:59
  82.6 249.8 %all-reduce.6.cloned.1.call-start = ((), (), s32[]{:S(2)}) async-start(), calls=%async_computation.2 | async-start | bytes 8388608 | tf_op jit(solution)/shard_map/psum | solution.py:59
  342.3 1.9 copy-start
Sparse Core Ops, SparseCore 0:
  82.7 92.0 all-reduce.3
  177.2 155.1 all-reduce.5
